TPU v7x, 256 devices: a whole 4x4x8 slice. The times are simulated.
256 devices in a mesh: sub: 4 (over z_hi, core), gx: 64 (over x, z_lo, y).
Axes of the slice: x: 4, y: 4, z: 8 (z_hi: 2, z_lo: 4; z = z_hi * 4 + z_lo), core: 2. Of those that a mesh axis runs over, the one named last changes fastest.
Arguments:
- value_field: float32 [8, 512, 256, 256], P('sub', 'gx'), may hold values from -6 to 6
- speed_field: float32 [8, 512, 256, 256], P('sub', 'gx'), may hold values from 0.25 to 2
- drift_matrix: float32 [8, 3, 3], P('sub'), may hold values from -0.5 to 0.5
- drift_offset: float32 [8, 3], P('sub'), may hold values from -0.5 to 0.5
- control_bound: float32 [8, 3], P('sub'), may hold values from 0.5 to 1
- partner_table: int32 [8], replicated, may hold values from 0 to 7, as said below
- dropped_dim: int32 [8], P('sub'), may hold values from 1 to 2, as said below
Outputs:
- final_value: float32 [8, 512, 256, 256], P('sub', 'gx')
- shared_plane: float32 [8, 512, 256], P('sub', 'gx')
Inputs may be any that keep to these rules, and one draw needn't show every extreme that they name: `partner_table`: a permutation of the 8 subsystems that forms a single cycle through all of them, so no subsystem is its own partner. `dropped_dim`: half of the subsystems drop dimension 1 and half dimension 2.
All inputs are finite; a program needn't handle non-finite values.
Results may differ from a plain program's by a relative error of at most 0.00075.
Values sent between devices are 32-bit elements; how exact they have to be, the bound alone decides.
A program may use at most 128 MiB of HBM per device.

v0:
```python
import jax
import jax.numpy as jnp
from jax import lax
from jax.sharding import PartitionSpec as P

STEPS = 2


def padded_2(cells, sides, width):
    for axis, dim in sides:
        count = lax.axis_size(axis)
        head = lax.slice_in_dim(cells, 0, width, axis=dim)
        tail = lax.slice_in_dim(cells, cells.shape[dim] - width, cells.shape[dim], axis=dim)
        cells = jnp.concatenate(
            [
                lax.ppermute(tail, axis, [(i, (i + 1) % count) for i in range(count)]),
                cells,
                lax.ppermute(head, axis, [((i + 1) % count, i) for i in range(count)]),
            ],
            axis=dim,
        )
    return cells


def from_everyone(array, axis):
    copies = jnp.broadcast_to(array, (lax.axis_size(axis), *array.shape))
    return lax.all_to_all(copies, axis, split_axis=0, concat_axis=0, tiled=True)


def joined_along(tiles, dim):
    tiles = jnp.moveaxis(tiles, 0, dim)
    dims = tiles.shape
    return tiles.reshape(*dims[:dim], dims[dim] * dims[dim + 1], *dims[dim + 2 :])


def gathered_copies(array, axis, dim):
    tiles = from_everyone(array, axis)
    return joined_along(tiles, dim)


def smaller(first, second):
    return jnp.where(jnp.abs(first) <= jnp.abs(second), first, second)


def one_sided(extended, dim_index, step_size):
    cell_count = extended.shape[dim_index] - 4

    def shifted(offset):
        return lax.slice_in_dim(extended, 2 + offset, 2 + offset + cell_count, axis=dim_index)

    back_two = shifted(-2)
    back_one = shifted(-1)
    middle = shifted(0)
    ahead_one = shifted(1)
    ahead_two = shifted(2)
    curve_back = back_two - 2.0 * back_one + middle
    curve_mid = back_one - 2.0 * middle + ahead_one
    curve_ahead = middle - 2.0 * ahead_one + ahead_two
    minus_side = (middle - back_one) / step_size + smaller(curve_back, curve_mid) / (
        2.0 * step_size
    )
    plus_side = (ahead_one - middle) / step_size - smaller(curve_mid, curve_ahead) / (
        2.0 * step_size
    )
    return (minus_side, plus_side)


def coordinates(first_row, cell_count, total_cells):
    indices = (first_row + jnp.arange(cell_count, dtype=jnp.int32)) % total_cells
    return -1.0 + (indices.astype(jnp.float32) + 0.5) * (2.0 / total_cells)


def advance(
    extended,
    speed_rows,
    first_coords,
    drift_matrix,
    drift_offset,
    control_bound,
    spacing,
    time_step,
):
    row_count = extended.shape[1] - 4
    grid_cells = extended.shape[2]
    center = lax.slice_in_dim(extended, 2, 2 + row_count, axis=1)
    gradients = [one_sided(extended, 1, spacing[0])]
    padded = jnp.pad(center, ((0, 0), (0, 0), (2, 2), (0, 0)), mode="edge")
    gradients.append(one_sided(padded, 2, spacing[1]))
    padded = jnp.pad(center, ((0, 0), (0, 0), (0, 0), (2, 2)), mode="edge")
    gradients.append(one_sided(padded, 3, spacing[2]))
    second_axis = coordinates(0, grid_cells, grid_cells)
    third_axis = coordinates(0, extended.shape[3], extended.shape[3])
    positions = (
        first_coords[None, :, None, None],
        second_axis[None, None, :, None],
        third_axis[None, None, None, :],
    )
    hamiltonian = jnp.zeros_like(center)
    for d in range(3):
        drift_term = drift_offset[:, d][:, None, None, None]
        for e in range(3):
            drift_term = drift_term + drift_matrix[:, d, e][:, None, None, None] * positions[e]
        minus_side, plus_side = gradients[d]
        average = 0.5 * (minus_side + plus_side)
        reach = control_bound[:, d][:, None, None, None] * speed_rows
        hamiltonian = (
            hamiltonian
            + drift_term * average
            - reach * jnp.abs(average)
            - (jnp.abs(drift_term) + reach) * 0.5 * (plus_side - minus_side)
        )
    return jnp.minimum(center, center - time_step * hamiltonian)


def on_device(
    value_field, speed_field, drift_matrix, drift_offset, control_bound, partner_table, dropped_dim
):
    local_subs = value_field.shape[0]
    local_rows = value_field.shape[1]
    grid_cells = value_field.shape[2]
    total_rows = local_rows * lax.axis_size("gx")
    spacing = (2.0 / total_rows, 2.0 / grid_cells, 2.0 / value_field.shape[3])
    time_step = min(spacing) / 15.0
    row_start = lax.axis_index("gx") * local_rows
    current = value_field
    first_coords = coordinates(row_start, local_rows, total_rows)
    for repeat in range(STEPS):
        extended = padded_2(current, (("gx", 1),), 2)
        current = advance(
            extended,
            speed_field,
            first_coords,
            drift_matrix,
            drift_offset,
            control_bound,
            spacing,
            time_step,
        )
    min_second = jnp.min(current, axis=2)
    min_third = jnp.min(current, axis=3)
    own_plane = jnp.where((dropped_dim == 1)[:, None, None], min_second, min_third)
    gathered = gathered_copies(own_plane, "sub", 0)
    own_index = lax.axis_index("sub") * local_subs + jnp.arange(local_subs, dtype=jnp.int32)
    wanted = partner_table[own_index]
    selector = wanted[:, None] == jnp.arange(gathered.shape[0], dtype=jnp.int32)[None, :]
    partner_plane = jnp.sum(jnp.where(selector[:, :, None, None], gathered[None], 0.0), axis=1)
    return (current, jnp.maximum(own_plane, partner_plane))


def solution(mesh):
    return jax.shard_map(
        on_device,
        mesh=mesh,
        in_specs=(
            P("sub", "gx", None, None),
            P("sub", "gx", None, None),
            P("sub", None, None),
            P("sub", None),
            P("sub", None),
            P(),
            P("sub"),
        ),
        out_specs=(P("sub", "gx", None, None), P("sub", "gx", None)),
        check_vma=False,
    )
```

profile of v0, /device:TPU:1, one launch (start us, length us, event | category | flops | bytes accessed | tf_op | source)
XLA Modules:
  0.0 169.5 jit_solution(12855246917814613128)
XLA Ops:
  0.6 6.7 %constant_dynamic-update-slice_fusion.1 = (f32[2,10,256,256]{3,1,0,2:T(8,128)}, f32[2,8,256,256]{3,1,0,2:T(8,128)S(1)}) fusion(f32[2,8,256,256]{3,2,1,0:T(8,128)} %param.7), kind=kLoop, calls=%fused_computation.134 | loop fusion | bytes 12582912
  7.3 1.9 %fusion.71 = (f32[2,2,256,256]{3,1,0,2:T(2,128)}, f32[2,2,256,256]{3,1,0,2:T(2,128)}) fusion(f32[2,8,256,256]{3,1,0,2:T(8,128)S(1)} %get-tuple-element.37), kind=kLoop, calls=%fused_computation.179 | loop fusion | bytes 4194304 | tf_op jit(solution)/shard_map/slice | solution.py:13
  9.3 9.8 %collective-permute-start.1 = (f32[2,2,256,256]{3,1,0,2:T(2,128)}, f32[2,2,256,256]{3,1,0,2:T(2,128)}, u32[]{:S(2)}, u32[]{:S(2)}) collective-permute-start(f32[2,2,256,256]{3,1,0,2:T(2,128)} %get-tuple-element.35), channel_id=1, source_target_pairs={{1,0},{2,1},{3,2},{4,3},{5,4},{6,5},{7,6},{8,7},{9,8},{10,9},{11,1... | collective-permute-start | bytes 3145736 | tf_op jit(solution)/shard_map/ppermute | solution.py:18
  19.1 2.1 %fusion.72 = (f32[2,8,256,1]{3,2,1,0:T(8,128)}, f32[2,8,256,1]{3,2,1,0:T(8,128)S(1)}) fusion(f32[2,8,256,256]{3,2,1,0:T(8,128)S(1)} %copy-done.4), kind=kLoop, calls=%fused_computation.180 | loop fusion | bytes 65536 | tf_op jit(solution)/shard_map/jit(_pad)/slice | solution.py:89
  22.0 0.8 copy.153
  22.9 2.2 %copy.173 = f32[2,8,256,1]{2,1,0,3:T(8,128)S(1)} copy(f32[2,8,256,1]{3,2,1,0:T(8,128)} %get-tuple-element.40) | data formatting | bytes 32768
  26.4 0.7 slice_bitcast_fusion.3
  27.4 1.5 broadcast_add_fusion
  29.0 12.3 %collective-permute-done.1 = f32[2,2,256,256]{3,1,0,2:T(2,128)} collective-permute-done((f32[2,2,256,256]{3,1,0,2:T(2,128)}, f32[2,2,256,256]{3,1,0,2:T(2,128)}, u32[]{:S(2)}, u32[]{:S(2)}) %collective-permute-start.1) | collective-permute-done | bytes 1048608 | tf_op jit(solution)/shard_map/ppermute | solution.py:18
  41.2 2.6 %constant_dynamic-update-slice_fusion = f32[2,10,256,256]{3,1,0,2:T(8,128)} fusion(f32[2,10,256,256]{3,1,0,2:T(8,128)} %get-tuple-element.36, f32[2,2,256,256]{3,1,0,2:T(2,128)} %collective-permute-done.1), kind=kLoop, calls=%fused_computation.133 | loop fusion | bytes 2097152 | tf_op jit(solution)/shard_map/concatenate | solution.py:14
  43.9 5.3 %collective-permute-done = f32[2,2,256,256]{3,1,0,2:T(2,128)} collective-permute-done((f32[2,2,256,256]{3,1,0,2:T(2,128)}, f32[2,2,256,256]{3,1,0,2:T(2,128)}, u32[]{:S(2)}, u32[]{:S(2)}) %collective-permute-start) | collective-permute-done | bytes 1048608 | tf_op jit(solution)/shard_map/ppermute | solution.py:16
  49.2 1.9 %reshape.504 = f32[2,8,256,2]{3,1,0,2:T(8,128)} broadcast(f32[2,8,256]{1,0,2:T(2,128)S(1)} %copy.155), dimensions={0,1,2} | broadcast | bytes 49152 | tf_op jit(solution)/shard_map/jit(_pad)/reshape | solution.py:89
  51.1 2.0 %reshape.505 = f32[2,8,256,2]{3,1,0,2:T(8,128)} broadcast(f32[2,8,256]{1,0,2:T(2,128)S(1)} %copy.160), dimensions={0,1,2} | broadcast | bytes 49152 | tf_op jit(solution)/shard_map/jit(_pad)/reshape | solution.py:89
  53.1 30.2 %subtract_minimum_fusion.1 = f32[2,8,256,256]{3,1,0,2:T(8,128)S(1)} fusion(f32[2,8,256,256]{3,1,0,2:T(8,128)} %copy-done.3, f32[2,8,256,2]{3,1,0,2:T(8,128)} %reshape.505, f32[2,8,256,2]{3,1,0,2:T(8,128)} %reshape.504, f32[2,8,2,256]{3,1,0,2:T(8,128)S(1)} %reshape.503, f32[2,8,2,256]{3,1,0,2:T(8,128)S(1)} %reshape.502, ...), kind=kLoop, calls=%fused_computation.25 | loop fusion | flops 133169152 | bytes 22206488 | tf_op jit(solution)/shard_map/min | solution.py:112
  83.3 2.0 %copy-done.1 = f32[2,8,256,256]{3,1,0,2:T(8,128)} copy-done((f32[2,8,256,256]{3,1,0,2:T(8,128)}, f32[2,8,256,256]{3,1,0,2:T(8,128)S(1)}, u32[]{:S(2)}) %copy-start.1) | copy-done | bytes 4194328
  85.3 1.9 %fusion.69 = (f32[2,2,256,256]{3,1,0,2:T(2,128)}, f32[2,2,256,256]{3,1,0,2:T(2,128)}) fusion(f32[2,8,256,256]{3,1,0,2:T(8,128)S(1)} %subtract_minimum_fusion.1), kind=kLoop, calls=%fused_computation.177 | loop fusion | bytes 4194304 | tf_op jit(solution)/shard_map/slice | solution.py:13
  87.2 7.5 %collective-permute-start.3 = (f32[2,2,256,256]{3,1,0,2:T(2,128)}, f32[2,2,256,256]{3,1,0,2:T(2,128)}, u32[]{:S(2)}, u32[]{:S(2)}) collective-permute-start(f32[2,2,256,256]{3,1,0,2:T(2,128)} %get-tuple-element.29), channel_id=1, source_target_pairs={{1,0},{2,1},{3,2},{4,3},{5,4},{6,5},{7,6},{8,7},{9,8},{10,9},{11,1... | collective-permute-start | bytes 3145736 | tf_op jit(solution)/shard_map/ppermute | solution.py:18
  94.7 0.6 gather_fusion
  95.4 4.3 %fusion.70 = (f32[2,8,256,1]{3,1,0,2:T(8,128)}, f32[2,8,256,1]{3,1,0,2:T(8,128)S(1)}) fusion(f32[2,8,256,256]{3,1,0,2:T(8,128)} %copy-done.1), kind=kLoop, calls=%fused_computation.178 | loop fusion | bytes 65536 | tf_op jit(solution)/shard_map/jit(_pad)/slice | solution.py:89
  99.6 2.5 %copy.167 = f32[2,8,256,1]{2,1,0,3:T(8,128)S(1)} copy(f32[2,8,256,1]{3,1,0,2:T(8,128)} %get-tuple-element.32) | data formatting | bytes 32768 | tf_op jit(solution)/shard_map/jit(_pad)/slice | solution.py:89
  102.1 0.8 copy.168
  103.0 1.1 copy.169
  104.1 0.8 copy.170
  104.9 0.9 slice_bitcast_fusion.1
  105.8 10.7 %collective-permute-done.2 = f32[2,2,256,256]{3,1,0,2:T(2,128)} collective-permute-done((f32[2,2,256,256]{3,1,0,2:T(2,128)}, f32[2,2,256,256]{3,1,0,2:T(2,128)}, u32[]{:S(2)}, u32[]{:S(2)}) %collective-permute-start.2) | collective-permute-done | bytes 1048608 | tf_op jit(solution)/shard_map/ppermute | solution.py:16
  116.4 2.9 %reshape.508 = f32[2,8,256,2]{3,1,0,2:T(8,128)} broadcast(f32[2,8,256]{1,0,2:T(2,128)} %copy.168), dimensions={0,1,2} | broadcast | bytes 49152 | tf_op jit(solution)/shard_map/jit(_pad)/reshape | solution.py:89
  119.3 2.9 %reshape.509 = f32[2,8,256,2]{3,1,0,2:T(8,128)} broadcast(f32[2,8,256]{1,0,2:T(2,128)} %copy.170), dimensions={0,1,2} | broadcast | bytes 49152 | tf_op jit(solution)/shard_map/jit(_pad)/reshape | solution.py:89
  122.2 29.2 %fusion.68 = (f32[2,8,256]{1,0,2:T(2,128)}, f32[2,8,256]{2,1,0:T(8,128)S(1)}, f32[2,8,256,256]{3,1,0,2:T(8,128)}) fusion(f32[2,8,256,256]{3,1,0,2:T(8,128)S(1)} %copy-done.2, f32[2]{0:T(128)S(1)} %get-tuple-element.25, f32[2,8,256,2]{3,1,0,2:T(8,128)} %reshape.509, f32[2,8,256,2]{3,1,0,2:T(8,128)} %reshape.508, f32[2,256]{1,0:T(2,128)S(1)} %get-tuple-element.47, ...), kind=kLoop, calls=%fused_computation.176 | loop fusion | flops 137355264 | bytes 14899224 | tf_op jit(solution)/shard_map/reduce_min | solution.py:140
  151.4 1.0 copy.171
  152.5 0.7 broadcast_in_dim.58
  153.2 8.4 %all-to-all-start = ((f32[4,2,8,256]{3,2,1,0:T(8,128)}), f32[4,2,8,256]{3,2,1,0:T(8,128)S(1)}, u32[]{:S(2)}, u32[]{:S(2)}) async-start(f32[4,2,8,256]{3,2,1,0:T(8,128)} %broadcast_in_dim.58), calls=%async_computation | async-start | bytes 131072 | tf_op jit(solution)/shard_map/all_to_all | solution.py:27
  161.7 6.6 %copy.172 = f32[2,8,256,256]{3,2,1,0:T(8,128)} copy(f32[2,8,256,256]{3,1,0,2:T(8,128)} %get-tuple-element.27) | data formatting | bytes 8388608
  (45 shorter events, 3.8 us)
Async XLA Ops:
  0.6 94.1 %copy-start = (s32[8]{0:T(128)S(1)}, s32[8]{0:T(128)}, u32[]{:S(2)}) copy-start(s32[8]{0:T(128)} %param.12) | copy-start | bytes 100
  7.3 13.9 %copy-start.3 = (f32[2,8,256,256]{3,1,0,2:T(8,128)}, f32[2,8,256,256]{3,1,0,2:T(8,128)S(1)}, u32[]{:S(2)}) copy-start(f32[2,8,256,256]{3,1,0,2:T(8,128)S(1)} %get-tuple-element.37) | copy-start | bytes 12582916
  7.3 11.8 %copy-start.4 = (f32[2,8,256,256]{3,2,1,0:T(8,128)S(1)}, f32[2,8,256,256]{3,2,1,0:T(8,128)}, u32[]{:S(2)}) copy-start(f32[2,8,256,256]{3,2,1,0:T(8,128)} %param.7) | copy-start | bytes 12582916
  9.3 32.0 %collective-permute-start.1 = (f32[2,2,256,256]{3,1,0,2:T(2,128)}, f32[2,2,256,256]{3,1,0,2:T(2,128)}, u32[]{:S(2)}, u32[]{:S(2)}) collective-permute-start(f32[2,2,256,256]{3,1,0,2:T(2,128)} %get-tuple-element.35), channel_id=1, source_target_pairs={{1,0},{2,1},{3,2},{4,3},{5,4},{6,5},{7,6},{8,7},{9,8},{10,9},{11,1... | collective-permute-start | bytes 3145736 | tf_op jit(solution)/shard_map/ppermute | solution.py:18
  19.1 30.1 %collective-permute-start = (f32[2,2,256,256]{3,1,0,2:T(2,128)}, f32[2,2,256,256]{3,1,0,2:T(2,128)}, u32[]{:S(2)}, u32[]{:S(2)}) collective-permute-start(f32[2,2,256,256]{3,1,0,2:T(2,128)} %get-tuple-element.34), channel_id=1, source_target_pairs={{0,1},{1,2},{2,3},{3,4},{4,5},{5,6},{6,7},{7,8},{8,9},{9,10},{10,1... | collective-permute-start | bytes 3145736 | tf_op jit(solution)/shard_map/ppermute | solution.py:16
  19.1 2.2 %copy-start.5 = (f32[2,3,3]{2,0,1:T(2,128)S(1)}, f32[2,3,3]{2,0,1:T(2,128)}, u32[]{:S(2)}) copy-start(f32[2,3,3]{2,0,1:T(2,128)} %param.9) | copy-start | bytes 220
  19.1 2.4 %copy-start.6 = (f32[2,3]{1,0:T(2,128)S(1)}, f32[2,3]{1,0:T(2,128)}, u32[]{:S(2)}) copy-start(f32[2,3]{1,0:T(2,128)} %param.10) | copy-start | bytes 76
  21.3 4.8 %copy-start.7 = (f32[2,3]{1,0:T(2,128)S(1)}, f32[2,3]{1,0:T(2,128)}, u32[]{:S(2)}) copy-start(f32[2,3]{1,0:T(2,128)} %param.11) | copy-start | bytes 76
  83.3 2.0 %copy-start.1 = (f32[2,8,256,256]{3,1,0,2:T(8,128)}, f32[2,8,256,256]{3,1,0,2:T(8,128)S(1)}, u32[]{:S(2)}) copy-start(f32[2,8,256,256]{3,1,0,2:T(8,128)S(1)} %subtract_minimum_fusion.1) | copy-start | bytes 12582916
  85.3 10.1 %copy-start.8 = (s32[2]{0:T(128)S(1)}, s32[2]{0:T(128)}, u32[]{:S(2)}) copy-start(s32[2]{0:T(128)} %param.13) | copy-start | bytes 28
  87.2 29.2 %collective-permute-start.2 = (f32[2,2,256,256]{3,1,0,2:T(2,128)}, f32[2,2,256,256]{3,1,0,2:T(2,128)}, u32[]{:S(2)}, u32[]{:S(2)}) collective-permute-start(f32[2,2,256,256]{3,1,0,2:T(2,128)} %get-tuple-element.28), channel_id=1, source_target_pairs={{0,1},{1,2},{2,3},{3,4},{4,5},{5,6},{6,7},{7,8},{8,9},{9,10},{10,1... | collective-permute-start | bytes 3145736 | tf_op jit(solution)/shard_map/ppermute | solution.py:16
  87.2 29.2 %collective-permute-start.3 = (f32[2,2,256,256]{3,1,0,2:T(2,128)}, f32[2,2,256,256]{3,1,0,2:T(2,128)}, u32[]{:S(2)}, u32[]{:S(2)}) collective-permute-start(f32[2,2,256,256]{3,1,0,2:T(2,128)} %get-tuple-element.29), channel_id=1, source_target_pairs={{1,0},{2,1},{3,2},{4,3},{5,4},{6,5},{7,6},{8,7},{9,8},{10,9},{11,1... | collective-permute-start | bytes 3145736 | tf_op jit(solution)/shard_map/ppermute | solution.py:18
  104.9 17.3 %copy-start.2 = (f32[2,8,256,256]{3,1,0,2:T(8,128)S(1)}, f32[2,8,256,256]{3,1,0,2:T(8,128)}, u32[]{:S(2)}) copy-start(f32[2,8,256,256]{3,1,0,2:T(8,128)} %copy-done.1) | copy-start | bytes 12582916
  153.2 15.6 %all-to-all-start = ((f32[4,2,8,256]{3,2,1,0:T(8,128)}), f32[4,2,8,256]{3,2,1,0:T(8,128)S(1)}, u32[]{:S(2)}, u32[]{:S(2)}) async-start(f32[4,2,8,256]{3,2,1,0:T(8,128)} %broadcast_in_dim.58), calls=%async_computation | async-start | bytes 131072 | tf_op jit(solution)/shard_map/all_to_all | solution.py:27
where the time goes:
time: 170 us; the launch traced here: 169 us
  other arithmetic  62.2 us (37%)
  local copies, waits for them, and re-layouts  52.1 us (31%)
  waiting for transfers between devices  28.7 us (17%)
  starting transfers between devices  25.7 us (15%)
    min x1, other arithmetic, advance(): return jnp.minimum(center, center - time_step * hamiltonian)  30.2 us
    reduce_min x1, other arithmetic, on_device(): min_third = jnp.min(current, axis=3)  29.2 us
    unnamed x22, local copies, waits for them, and re-layouts  18.2 us
    ppermute x2, starting transfers between devices, padded_2(): lax.ppermute(head, axis, [((i + 1) % count, i) for i in range(count)])  17.3 us
    ppermute x2, waiting for transfers between devices, padded_2(): lax.ppermute(tail, axis, [(i, (i + 1) % count) for i in range(count)])  16 us
    ppermute x2, waiting for transfers between devices, padded_2(): lax.ppermute(head, axis, [((i + 1) % count, i) for i in range(count)])  12.3 us
    slice x8, local copies, waits for them, and re-layouts, advance(): padded = jnp.pad(center, ((0, 0), (0, 0), (0, 0), (2, 2)), mode='edge')  12 us
    reshape x4, local copies, waits for them, and re-layouts, advance(): padded = jnp.pad(center, ((0, 0), (0, 0), (0, 0), (2, 2)), mode='edge')  9.68 us
  transfers between devices with their start and end apart: 5, of which 4 were waited for; matrix products, arithmetic and copies ran while one was open for 18% of the time, Pallas kernels for 0%

commit v1 on v0

v1 whole, which is shorter than its diff:
```python
import functools

import jax
import jax.numpy as jnp
from jax import lax
from jax.experimental import pallas as pl
from jax.experimental.pallas import tpu as pltpu
from jax.sharding import PartitionSpec as P

STEPS = 2
LANES = 128
PAD = 8
TS = 16
BLOCKS = 4


def pick(a, abs_a, b, abs_b):
    return jnp.where(abs_a <= abs_b, a, b)


def kernel(
    dims,
    value_hbm,
    speed_hbm,
    matrix_hbm,
    offset_hbm,
    bound_hbm,
    partner_hbm,
    dropped_hbm,
    final,
    shared_ref,
    first,
    second,
    speed,
    drift_matrix,
    drift_offset,
    control_bound,
    partner_table,
    dropped_dim,
    low_second,
    low_third,
    own,
    gathered,
    load_sem,
    scalar_sem,
    send_sem,
    recv_sem,
    plane_send,
    plane_recv,
):
    subs, rows, cells, halves, sub_count, ring, total_rows = dims
    block = cells // BLOCKS
    chunks = subs * BLOCKS
    sub_at = lax.axis_index("sub")
    at = lax.axis_index("gx")
    right = lax.rem(at + 1, ring)
    left = lax.rem(at + ring - 1, ring)
    peers = [lax.rem(sub_at + k, sub_count) for k in range(1, sub_count)]

    spacing = (2.0 / total_rows, 2.0 / cells, 2.0 / (halves * LANES))
    time_step = min(spacing) / 15.0
    scale = tuple(time_step / (2.0 * h) for h in spacing)

    barrier = pltpu.get_barrier_semaphore()
    for target in (left, right):
        pl.semaphore_signal(barrier, inc=1, device_id={"gx": target}, device_id_type=pl.DeviceIdType.MESH)
    for target in peers:
        pl.semaphore_signal(barrier, inc=1, device_id={"sub": target}, device_id_type=pl.DeviceIdType.MESH)

    def loads():
        out = []
        for s in range(subs):
            for h in range(halves):
                lanes = pl.ds(h * LANES, LANES)
                out.append(
                    pltpu.make_async_copy(
                        value_hbm.at[s, :, :, lanes],
                        first.at[s, pl.ds(2, rows), h, pl.ds(PAD, cells), :],
                        load_sem.at[0, s, h],
                    )
                )
                out.append(
                    pltpu.make_async_copy(
                        speed_hbm.at[s, :, :, lanes], speed.at[s, :, h], load_sem.at[1, s, h]
                    )
                )
        for k, (source, held) in enumerate(
            (
                (matrix_hbm, drift_matrix),
                (offset_hbm, drift_offset),
                (bound_hbm, control_bound),
                (partner_hbm, partner_table),
                (dropped_hbm, dropped_dim),
            )
        ):
            out.append(pltpu.make_async_copy(source, held, scalar_sem.at[k]))
        return out

    for copy in loads():
        copy.start()
    pl.semaphore_wait(barrier, 2 + len(peers))

    def rim_copies(step, chunk):
        s = chunk // BLOCKS
        j = lax.rem(chunk, BLOCKS) * block
        out = []
        for way, (source_row, target_row, target) in enumerate(
            ((rows - 2, 0, right), (0, rows + 2, left))
        ):
            for h in range(halves):
                if step == 0:
                    source = value_hbm.at[
                        s, pl.ds(source_row, 2), pl.ds(j, block), pl.ds(h * LANES, LANES)
                    ]
                    held = first
                else:
                    source = second.at[s, pl.ds(source_row + 2, 2), h, pl.ds(PAD + j, block), :]
                    held = second
                out.append(
                    pltpu.make_async_remote_copy(
                        src_ref=source,
                        dst_ref=held.at[s, pl.ds(target_row, 2), h, pl.ds(PAD + j, block), :],
                        send_sem=send_sem.at[step, way, chunk, h],
                        recv_sem=recv_sem.at[step, way, chunk, h],
                        device_id={"gx": target},
                        device_id_type=pl.DeviceIdType.MESH,
                    )
                )
        return out

    @pl.loop(0, chunks)
    def _(chunk):
        for copy in rim_copies(0, chunk):
            copy.start()

    for copy in loads():
        copy.wait()

    def repeat_ends(held):
        @pl.loop(0, subs * rows)
        def _(i):
            s = i // rows
            r = lax.rem(i, rows) + 2
            for h in range(halves):
                for cell, start in ((PAD, PAD - 2), (PAD + cells - 1, PAD + cells)):
                    held[s, r, h, pl.ds(start, 2), :] = jnp.broadcast_to(
                        held[s, r, h, pl.ds(cell, 1), :], (2, LANES)
                    )

    repeat_ends(first)
    lane = lax.broadcasted_iota(jnp.int32, (TS, LANES), 1)
    at_start = lane == 0
    at_end = lane == LANES - 1
    low_third[...] = jnp.zeros_like(low_third)
    low_second[...] = jnp.full_like(low_second, jnp.inf)

    def coordinate(index, total):
        return -1.0 + (index.astype(jnp.float32) + 0.5) * (2.0 / total)

    def ahead(parts, edge):
        turned = [pltpu.roll(p, LANES - 1, 1) for p in parts]
        return [
            jnp.where(at_end, turned[h + 1] if h + 1 < halves else edge, turned[h])
            for h in range(halves)
        ]

    def behind(parts, edge):
        turned = [pltpu.roll(p, 1, 1) for p in parts]
        return [
            jnp.where(at_start, turned[h - 1] if h > 0 else edge, turned[h]) for h in range(halves)
        ]

    def cells_of(held, step, s, groups, start):
        matrix = [[drift_matrix[d, s, e] * scale[d] for e in range(3)] for d in range(3)]
        offset = [drift_offset[s, d] * scale[d] for d in range(3)]
        bound = [control_bound[s, d] * scale[d] for d in range(3)]
        index = start + lax.broadcasted_iota(jnp.int32, (TS, LANES), 0)
        second_axis = coordinate(index, cells)
        drift_base = []
        for h in range(halves):
            third_axis = coordinate(lane + h * LANES, halves * LANES)
            drift_base.append(
                [matrix[d][1] * second_axis + matrix[d][2] * third_axis for d in range(3)]
            )
        lows = None
        for low_row, high_row in groups:

            def value(r, h, shift=0):
                return held[s, r + 2, h, pl.ds(PAD + start + shift, TS), :]

            middle = {r: [value(r, h) for h in range(halves)] for r in range(low_row - 2, high_row + 2)}
            along_first = {}
            for h in range(halves):
                slope = {r: middle[r + 1][h] - middle[r][h] for r in range(low_row - 2, high_row + 1)}
                curve = {r: slope[r] - slope[r - 1] for r in range(low_row - 1, high_row + 1)}
                size = {r: jnp.abs(curve[r]) for r in curve}
                for r in range(low_row - 1, high_row):
                    face = pick(curve[r], size[r], curve[r + 1], size[r + 1])
                    twice = slope[r] + slope[r]
                    along_first[r, h, 0] = twice - face
                    along_first[r + 1, h, 1] = -(twice + face)
            for r in range(low_row, high_row):
                x0 = -1.0 + ((at * rows + r).astype(jnp.float32) + 0.5) * (2.0 / total_rows)
                center = middle[r]
                up = ahead(center, center[halves - 1])
                down = behind(center, center[0])
                plus = [up[h] - center[h] for h in range(halves)]
                minus = [down[h] - center[h] for h in range(halves)]
                curve = [plus[h] + minus[h] for h in range(halves)]
                curve_up = ahead(curve, 0.0)
                curve_down = behind(curve, 0.0)
                results = []
                for h in range(halves):
                    sides = [(along_first[r, h, 0], along_first[r, h, 1])]
                    a2, a1, b1, b2 = (value(r, h, k) for k in (-2, -1, 1, 2))
                    p = b1 - center[h]
                    m = a1 - center[h]
                    c = p + m
                    c_up = (b2 - b1) - p
                    c_down = (a2 - a1) - m
                    size, size_up, size_down = jnp.abs(c), jnp.abs(c_up), jnp.abs(c_down)
                    sides.append(
                        (
                            (p + p) - pick(c, size, c_up, size_up),
                            (m + m) - pick(c_down, size_down, c, size),
                        )
                    )
                    c, c_up, c_down = curve[h], curve_up[h], curve_down[h]
                    size, size_up, size_down = jnp.abs(c), jnp.abs(c_up), jnp.abs(c_down)
                    sides.append(
                        (
                            (plus[h] + plus[h]) - pick(c, size, c_up, size_up),
                            (minus[h] + minus[h]) - pick(c_down, size_down, c, size),
                        )
                    )
                    drifting = None
                    reaching = None
                    for d, (x, y) in enumerate(sides):
                        drift = drift_base[h][d] + (offset[d] + matrix[d][0] * x0)
                        term = jnp.abs(drift) * jnp.where(drift >= 0.0, y, x)
                        reach = bound[d] * jnp.maximum(x, y)
                        drifting = term if drifting is None else drifting + term
                        reaching = reach if reaching is None else reaching + reach
                    gain = drifting + speed[s, r, h, pl.ds(start, TS), :] * reaching
                    result = center[h] + jnp.minimum(gain, 0.0)
                    results.append(result)
                    if step == 0:
                        second[s, r + 2, h, pl.ds(PAD + start, TS), :] = result
                    else:
                        final[s, r, pl.ds(start, TS), pl.ds(h * LANES, LANES)] = result
                        low = result[:8]
                        for k in range(8, TS, 8):
                            low = jnp.minimum(low, result[k : k + 8])
                        low_second[s, r, h] = jnp.minimum(low_second[s, r, h], low)
                if step == 1:
                    joint = results[0]
                    for part in results[1:]:
                        joint = jnp.minimum(joint, part)
                    least = jnp.min(joint, axis=1, keepdims=True)
                    if lows is None:
                        lows = low_third[s, pl.ds(start, TS), :]
                    lows = jnp.where(lane == r, least, lows)
        if step == 1:
            low_third[s, pl.ds(start, TS), :] = lows

    def run(held, step, chunk, groups):
        s = chunk // BLOCKS
        j = lax.rem(chunk, BLOCKS) * block

        @pl.loop(0, block // TS)
        def _(t):
            cells_of(held, step, s, groups, pl.multiple_of(j + t * TS, TS))

    inner = ((2, rows - 2),)
    rims = ((0, 2), (rows - 2, rows))

    @pl.loop(0, chunks)
    def _(chunk):
        run(first, 0, chunk, inner)
        for copy in rim_copies(0, chunk):
            copy.wait_recv()
        run(first, 0, chunk, rims)
        for copy in rim_copies(1, chunk):
            copy.start()

    repeat_ends(second)

    @pl.loop(0, chunks)
    def _(chunk):
        run(second, 1, chunk, inner)
        for copy in rim_copies(1, chunk):
            copy.wait_recv()
        run(second, 1, chunk, rims)

    for s in range(subs):
        over_third = jnp.transpose(low_third[s])[:rows]
        for h in range(halves):
            over_second = jnp.min(low_second[s, :, h], axis=1)
            plane = jnp.where(
                dropped_dim[s] == 1, over_second, over_third[:, h * LANES : (h + 1) * LANES]
            )
            own[s, :, pl.ds(h * LANES, LANES)] = plane
            gathered[sub_at * subs + s, :, pl.ds(h * LANES, LANES)] = plane

    plane_copies = [
        pltpu.make_async_remote_copy(
            src_ref=own,
            dst_ref=gathered.at[pl.ds(sub_at * subs, subs)],
            send_sem=plane_send.at[k],
            recv_sem=plane_recv.at[k],
            device_id={"sub": target},
            device_id_type=pl.DeviceIdType.MESH,
        )
        for k, target in enumerate(peers)
    ]
    for copy in plane_copies:
        copy.start()

    @pl.loop(0, chunks)
    def _(chunk):
        for step in range(STEPS):
            for copy in rim_copies(step, chunk):
                copy.wait_send()

    for copy in plane_copies:
        copy.wait_recv()
    for s in range(subs):
        partner = partner_table[sub_at * subs + s]
        shared_ref[s] = jnp.maximum(own[s], gathered[partner])
    for copy in plane_copies:
        copy.wait_send()


def on_device(dims, value_field, speed_field, drift_matrix, *others):
    subs, rows, cells, halves, sub_count, ring, total_rows = dims
    chunks = subs * BLOCKS
    in_vmem = pl.BlockSpec(memory_space=pltpu.VMEM)
    held = pltpu.VMEM((subs, rows + 4, halves, cells + 2 * PAD, LANES), jnp.float32)
    whole = pltpu.VMEM((subs, rows, halves, cells, LANES), jnp.float32)
    return pl.pallas_call(
        functools.partial(kernel, dims),
        out_shape=(
            jax.ShapeDtypeStruct((subs, rows, cells, halves * LANES), jnp.float32),
            jax.ShapeDtypeStruct((subs, rows, cells), jnp.float32),
        ),
        in_specs=[pl.BlockSpec(memory_space=pltpu.HBM)] * 7,
        out_specs=(in_vmem, in_vmem),
        scratch_shapes=[
            held,
            held,
            whole,
            pltpu.SMEM((3, subs, 3), jnp.float32),
            pltpu.SMEM((subs, 3), jnp.float32),
            pltpu.SMEM((subs, 3), jnp.float32),
            pltpu.SMEM((sub_count * subs,), jnp.int32),
            pltpu.SMEM((subs,), jnp.int32),
            pltpu.VMEM((subs, rows, halves, 8, LANES), jnp.float32),
            pltpu.VMEM((subs, cells, LANES), jnp.float32),
            pltpu.VMEM((subs, rows, cells), jnp.float32),
            pltpu.VMEM((sub_count * subs, rows, cells), jnp.float32),
            pltpu.SemaphoreType.DMA((2, subs, halves)),
            pltpu.SemaphoreType.DMA((5,)),
            pltpu.SemaphoreType.DMA((STEPS, 2, chunks, halves)),
            pltpu.SemaphoreType.DMA((STEPS, 2, chunks, halves)),
            pltpu.SemaphoreType.DMA((sub_count - 1,)),
            pltpu.SemaphoreType.DMA((sub_count - 1,)),
        ],
        compiler_params=pltpu.CompilerParams(
            collective_id=0, has_side_effects=True, vmem_limit_bytes=48 * 1024 * 1024
        ),
        name="steps_and_planes",
    )(value_field, speed_field, jnp.transpose(drift_matrix, (1, 0, 2)), *others)


def solution(mesh):
    sub_count, ring = mesh.shape["sub"], mesh.shape["gx"]

    def whole(value_field, *others):
        total_subs, total_rows, cells, third = value_field.shape
        dims = (
            total_subs // sub_count,
            total_rows // ring,
            cells,
            third // LANES,
            sub_count,
            ring,
            total_rows,
        )
        step = jax.shard_map(
            functools.partial(on_device, dims),
            mesh=mesh,
            in_specs=(
                P("sub", "gx", None, None),
                P("sub", "gx", None, None),
                P("sub", None, None),
                P("sub", None),
                P("sub", None),
                P(),
                P("sub"),
            ),
            out_specs=(P("sub", "gx", None, None), P("sub", "gx", None)),
            check_vma=False,
        )
        return step(value_field, *others)

    return whole
```

time: 170 us -> 74.5 us (0.44)
  Pallas kernels: 0 us -> 67.7 us
  other arithmetic: 62.2 us -> 0 us
  local copies, waits for them, and re-layouts: 52.1 us -> 5.96 us
  waiting for transfers between devices: 28.7 us -> 0 us
  starting transfers between devices: 25.7 us -> 0 us
    pallas_call x0 -> x1, Pallas kernels: none -> 67.7 us  [on_device(): pl.pallas_call(functools.partial(kernel, dims), out_shape=(jax.ShapeDtype...]
    min x1 -> x0, other arithmetic: 30.2 us -> none  [advance(): return jnp.minimum(center, center - time_step * hamiltonian)]
    reduce_min x1 -> x0, other arithmetic: 29.2 us -> none  [on_device(): min_third = jnp.min(current, axis=3)]
    ppermute x4 -> x0, waiting for transfers between devices: 28.2 us -> none  [the longest x2 16 us: padded_2(): lax.ppermute(tail, axis, [(i, (i + 1) % count) for i in range(count)])]
    slice x15 -> x0, local copies, waits for them, and re-layouts: 18.1 us -> none  [the longest x8 12 us: advance(): padded = jnp.pad(center, ((0, 0), (0, 0), (0, 0), (2, 2)), mode='edge')]
    ppermute x4 -> x0, starting transfers between devices: 17.3 us -> none  [the longest x2 17.3 us: padded_2(): lax.ppermute(head, axis, [((i + 1) % count, i) for i in range(count)])]
    unnamed x22 -> x12, local copies, waits for them, and re-layouts: 18.2 us -> 5.96 us
    reshape x8 -> x0, local copies, waits for them, and re-layouts: 9.69 us -> none  [the longest x4 9.68 us: advance(): padded = jnp.pad(center, ((0, 0), (0, 0), (0, 0), (2, 2)), mode='edge')]
  transfers between devices with their start and end apart: 5 -> 0, of which waited for: 4 -> 0; matrix products, arithmetic and copies ran while one was open for 18% -> 0% of each run, Pallas kernels for 0% -> 0%
where the time goes in v1:
time: 74.5 us; the launch traced here: 74.4 us
  Pallas kernels  67.7 us (91%)
  local copies, waits for them, and re-layouts  5.96 us (8%)
    pallas_call x1, Pallas kernels, on_device(): pl.pallas_call(functools.partial(kernel, dims), out_shape=(jax.ShapeDtype...  67.7 us
    unnamed x12, local copies, waits for them, and re-layouts  5.96 us

profile of v1, /device:TPU:1, one launch (start us, length us, event | category | flops | bytes accessed | tf_op | source)
XLA Modules:
  0.0 74.4 jit_solution(5903666174822451697)
XLA Ops:
  0.6 0.0 copy-start
  0.6 0.7 copy-done
  1.3 0.0 copy-start.1
  1.3 0.7 copy-done.1
  2.0 0.0 copy-start.2
  2.0 0.7 copy-done.2
  2.7 0.0 copy-start.3
  2.7 0.7 copy-done.3
  3.3 0.0 copy-start.4
  3.3 0.7 copy-done.4
  4.0 67.7 %steps_and_planes.1 = (f32[2,8,256,256]{3,2,1,0:T(8,128)S(1)}, f32[2,8,256]{2,1,0:T(8,128)S(1)}) custom-call(f32[2,8,256,256]{3,2,1,0:T(8,128)} %value_hbm.1, f32[2,8,256,256]{3,2,1,0:T(8,128)} %speed_hbm.1, f32[3,2,3]{2,1,0:T(2,128)S(1)} %bitcast.1, f32[2,3]{1,0:T(2,128)S(1)} %copy-done.1, f32[2,3]{1,0:T(2,128)S(1)} %copy-done.2, s32[8]{0:T(128)S(1)} %copy-done.3, ...), custom_call_target="tpu_custom_call" | custom-call | tf_op jit(solution)/shard_map/steps_and_planes/pallas_call | solution.py:340
  71.7 2.0 %copy.11 = f32[2,8,256,256]{3,2,1,0:T(8,128)} copy(f32[2,8,256,256]{3,2,1,0:T(8,128)S(1)} %get-tuple-element.4) | data formatting | bytes 8388608
  73.8 0.6 copy.12
Async XLA Ops:
  0.6 0.7 copy-start
  1.3 0.7 copy-start.1
  2.0 0.7 copy-start.2
  2.7 0.7 copy-start.3
  3.3 0.7 copy-start.4

commit v2 on v1

--- a/solution.py
+++ b/solution.py
@@ -11,7 +11,7 @@
 LANES = 128
 PAD = 8
 TS = 16
-BLOCKS = 4
+BLOCKS = 8
 
 
 def pick(a, abs_a, b, abs_b):
@@ -67,23 +67,20 @@
     for target in peers:
         pl.semaphore_signal(barrier, inc=1, device_id={"sub": target}, device_id_type=pl.DeviceIdType.MESH)
 
-    def loads():
-        out = []
-        for s in range(subs):
-            for h in range(halves):
-                lanes = pl.ds(h * LANES, LANES)
-                out.append(
-                    pltpu.make_async_copy(
-                        value_hbm.at[s, :, :, lanes],
-                        first.at[s, pl.ds(2, rows), h, pl.ds(PAD, cells), :],
-                        load_sem.at[0, s, h],
-                    )
-                )
-                out.append(
-                    pltpu.make_async_copy(
-                        speed_hbm.at[s, :, :, lanes], speed.at[s, :, h], load_sem.at[1, s, h]
-                    )
-                )
+    def loads(source, held, first_row, pad, kind):
+        return [
+            pltpu.make_async_copy(
+                source.at[s, :, :, pl.ds(h * LANES, LANES)],
+                held.at[s, pl.ds(first_row, rows), h, pl.ds(pad, cells), :],
+                load_sem.at[kind, s, h],
+            )
+            for s in range(subs)
+            for h in range(halves)
+        ]
+
+    value_loads = loads(value_hbm, first, 2, PAD, 0)
+    other_loads = loads(speed_hbm, speed, 0, 0, 1) + [
+        pltpu.make_async_copy(source, held, scalar_sem.at[k])
         for k, (source, held) in enumerate(
             (
                 (matrix_hbm, drift_matrix),
@@ -92,11 +89,9 @@
                 (partner_hbm, partner_table),
                 (dropped_hbm, dropped_dim),
             )
-        ):
-            out.append(pltpu.make_async_copy(source, held, scalar_sem.at[k]))
-        return out
-
-    for copy in loads():
+        )
+    ]
+    for copy in value_loads + other_loads:
         copy.start()
     pl.semaphore_wait(barrier, 2 + len(peers))
 
@@ -107,33 +102,29 @@
         for way, (source_row, target_row, target) in enumerate(
             ((rows - 2, 0, right), (0, rows + 2, left))
         ):
-            for h in range(halves):
-                if step == 0:
-                    source = value_hbm.at[
-                        s, pl.ds(source_row, 2), pl.ds(j, block), pl.ds(h * LANES, LANES)
-                    ]
-                    held = first
-                else:
-                    source = second.at[s, pl.ds(source_row + 2, 2), h, pl.ds(PAD + j, block), :]
-                    held = second
-                out.append(
-                    pltpu.make_async_remote_copy(
-                        src_ref=source,
-                        dst_ref=held.at[s, pl.ds(target_row, 2), h, pl.ds(PAD + j, block), :],
-                        send_sem=send_sem.at[step, way, chunk, h],
-                        recv_sem=recv_sem.at[step, way, chunk, h],
-                        device_id={"gx": target},
-                        device_id_type=pl.DeviceIdType.MESH,
-                    )
+            held = first if step == 0 else second
+            cells_sent = pl.ds(PAD + j, block)
+            out.append(
+                pltpu.make_async_remote_copy(
+                    src_ref=held.at[s, pl.ds(source_row + 2, 2), :, cells_sent, :],
+                    dst_ref=held.at[s, pl.ds(target_row, 2), :, cells_sent, :],
+                    send_sem=send_sem.at[step, way, chunk],
+                    recv_sem=recv_sem.at[step, way, chunk],
+                    device_id={"gx": target},
+                    device_id_type=pl.DeviceIdType.MESH,
                 )
+            )
         return out
+
+    for copy in value_loads:
+        copy.wait()
 
     @pl.loop(0, chunks)
     def _(chunk):
         for copy in rim_copies(0, chunk):
             copy.start()
 
-    for copy in loads():
+    for copy in other_loads:
         copy.wait()
 
     def repeat_ends(held):
@@ -331,13 +322,29 @@
         copy.wait_send()
 
 
+def put_out(final, shared, final_out, shared_out, final_sem, shared_sem):
+    subs, rows = final.shape[:2]
+    pieces = final_sem.shape[1]
+    count = rows // pieces
+    copies = [pltpu.make_async_copy(shared, shared_out, shared_sem)]
+    for s in range(subs):
+        for k in range(pieces):
+            at = (s, pl.ds(k * count, count))
+            copies.append(pltpu.make_async_copy(final.at[at], final_out.at[at], final_sem.at[s, k]))
+    for copy in copies:
+        copy.start()
+    for copy in copies:
+        copy.wait()
+
+
 def on_device(dims, value_field, speed_field, drift_matrix, *others):
     subs, rows, cells, halves, sub_count, ring, total_rows = dims
     chunks = subs * BLOCKS
     in_vmem = pl.BlockSpec(memory_space=pltpu.VMEM)
     held = pltpu.VMEM((subs, rows + 4, halves, cells + 2 * PAD, LANES), jnp.float32)
     whole = pltpu.VMEM((subs, rows, halves, cells, LANES), jnp.float32)
-    return pl.pallas_call(
+    arrays = (value_field, speed_field, jnp.transpose(drift_matrix, (1, 0, 2)), *others)
+    results = pl.pallas_call(
         functools.partial(kernel, dims),
         out_shape=(
             jax.ShapeDtypeStruct((subs, rows, cells, halves * LANES), jnp.float32),
@@ -360,16 +367,25 @@
             pltpu.VMEM((sub_count * subs, rows, cells), jnp.float32),
             pltpu.SemaphoreType.DMA((2, subs, halves)),
             pltpu.SemaphoreType.DMA((5,)),
-            pltpu.SemaphoreType.DMA((STEPS, 2, chunks, halves)),
-            pltpu.SemaphoreType.DMA((STEPS, 2, chunks, halves)),
+            pltpu.SemaphoreType.DMA((STEPS, 2, chunks)),
+            pltpu.SemaphoreType.DMA((STEPS, 2, chunks)),
             pltpu.SemaphoreType.DMA((sub_count - 1,)),
             pltpu.SemaphoreType.DMA((sub_count - 1,)),
         ],
         compiler_params=pltpu.CompilerParams(
-            collective_id=0, has_side_effects=True, vmem_limit_bytes=48 * 1024 * 1024
+            collective_id=0, has_side_effects=True, vmem_limit_bytes=40 * 1024 * 1024
         ),
         name="steps_and_planes",
-    )(value_field, speed_field, jnp.transpose(drift_matrix, (1, 0, 2)), *others)
+    )(*(pltpu.with_memory_space_constraint(a, pltpu.HBM) for a in arrays))
+    return pl.pallas_call(
+        put_out,
+        out_shape=tuple(jax.ShapeDtypeStruct(r.shape, r.dtype) for r in results),
+        in_specs=[pl.BlockSpec(memory_space=pl.ANY)] * 2,
+        out_specs=(pl.BlockSpec(memory_space=pl.ANY),) * 2,
+        scratch_shapes=[pltpu.SemaphoreType.DMA((subs, 4)), pltpu.SemaphoreType.DMA],
+        compiler_params=pltpu.CompilerParams(vmem_limit_bytes=1024 * 1024),
+        name="put_out",
+    )(*results)
 
 
 def solution(mesh):

time: 74.5 us -> 70.4 us (0.945)
  local copies, waits for them, and re-layouts: 5.96 us -> 0 us
  Pallas kernels: 67.7 us -> 69.7 us
    unnamed x12 -> x0, local copies, waits for them, and re-layouts: 5.96 us -> none
    pallas_call x0 -> x1, Pallas kernels: none -> 2.09 us  [on_device(): pl.pallas_call(put_out, out_shape=tuple((jax.ShapeDtypeStruct(r.shape, r....]
where the time goes in v2:
time: 70.4 us; the launch traced here: 70.3 us
  Pallas kernels  69.7 us (99%)
    pallas_call x1, Pallas kernels, on_device(): pl.pallas_call(functools.partial(kernel, dims), out_shape=(jax.ShapeDtype...  67.6 us
    pallas_call x1, Pallas kernels, on_device(): pl.pallas_call(put_out, out_shape=tuple((jax.ShapeDtypeStruct(r.shape, r....  2.09 us

profile of v2, /device:TPU:1, one launch (start us, length us, event | category | flops | bytes accessed | tf_op | source)
XLA Modules:
  0.0 70.3 jit_solution(9994484237640336374)
XLA Ops:
  0.6 67.6 %steps_and_planes.1 = (f32[2,8,256,256]{3,2,1,0:T(8,128)S(1)}, f32[2,8,256]{2,1,0:T(8,128)S(1)}) custom-call(f32[2,8,256,256]{3,2,1,0:T(8,128)} %value_hbm.1, f32[2,8,256,256]{3,2,1,0:T(8,128)} %speed_hbm.1, f32[3,2,3]{2,1,0:T(2,128)} %bitcast.1, f32[2,3]{1,0:T(2,128)} %offset_hbm.1, f32[2,3]{1,0:T(2,128)} %bound_hbm.1, s32[8]{0:T(128)} %partner_hbm.1, ...), custom_call_target="tpu_custom_call" | custom-call | tf_op jit(solution)/shard_map/steps_and_planes/pallas_call | solution.py:347
  68.2 2.1 %put_out.1 = (f32[2,8,256,256]{3,2,1,0:T(8,128)}, f32[2,8,256]{2,1,0:T(8,128)}) custom-call(f32[2,8,256,256]{3,2,1,0:T(8,128)S(1)} %get-tuple-element.4.final, f32[2,8,256]{2,1,0:T(8,128)S(1)} %get-tuple-element.5.shared), custom_call_target="tpu_custom_call" | custom-call | tf_op jit(solution)/shard_map/put_out/pallas_call | solution.py:380

commit v3 on v2

v3 whole, which is shorter than its diff:
```python
import functools

import jax
import jax.numpy as jnp
from jax import lax
from jax.experimental import pallas as pl
from jax.experimental.pallas import tpu as pltpu
from jax.sharding import PartitionSpec as P

STEPS = 2
LANES = 128
PAD = 8
TS = 16
LINE = 4
LAG = 2
LEAD = 6
BLOCKS = 8


def pick(a, abs_a, b, abs_b):
    return jnp.where(abs_a <= abs_b, a, b)


def rank_of(sub):
    return sub + 1 - 2 * lax.rem(sub, 2)


def kernel(
    dims,
    value_hbm,
    speed_hbm,
    matrix_hbm,
    offset_hbm,
    bound_hbm,
    partner_hbm,
    dropped_hbm,
    final,
    shared_ref,
    first,
    second,
    speed,
    drift_matrix,
    drift_offset,
    control_bound,
    partner_table,
    dropped_dim,
    low_second,
    low_third,
    own,
    gathered,
    load_sem,
    scalar_sem,
    send_sem,
    recv_sem,
    plane_send,
    plane_recv,
    ready,
):
    subs, rows, cells, halves, sub_count, ring, total_rows = dims
    block = cells // BLOCKS
    chunks = subs * BLOCKS
    sub_at = lax.axis_index("sub")
    at = lax.axis_index("gx")
    right = lax.rem(at + 1, ring)
    left = lax.rem(at + ring - 1, ring)
    peers = [lax.rem(sub_at + k, sub_count) for k in range(1, sub_count)]

    spacing = (2.0 / total_rows, 2.0 / cells, 2.0 / (halves * LANES))
    time_step = min(spacing) / 15.0
    scale = tuple(time_step / (2.0 * h) for h in spacing)

    barrier = pltpu.get_barrier_semaphore()
    for target in (left, right):
        pl.semaphore_signal(barrier, inc=1, device_id={"gx": target}, device_id_type=pl.DeviceIdType.MESH)
    rank = rank_of(sub_at)
    for target in peers:

        @pl.when(rank_of(target) > rank)
        def _():
            pl.semaphore_signal(barrier, inc=1, device_id={"sub": target}, device_id_type=pl.DeviceIdType.MESH)

    def loads(source, held, spans, first_row, pad, kind):
        return [
            pltpu.make_async_copy(
                source.at[s, pl.ds(low, count), :, pl.ds(h * LANES, LANES)],
                held.at[s, pl.ds(first_row + low, count), h, pl.ds(pad, cells), :],
                load_sem.at[kind + k, s, h],
            )
            for k, (low, count) in enumerate(spans)
            for s in range(subs)
            for h in range(halves)
        ]

    rim_loads = loads(value_hbm, first, ((0, 2), (rows - 2, 2)), 2, PAD, 0)
    other_loads = loads(value_hbm, first, ((2, rows - 4),), 2, PAD, 2)
    other_loads += loads(speed_hbm, speed, ((0, rows),), 0, 0, 3)
    other_loads += [
        pltpu.make_async_copy(source, held, scalar_sem.at[k])
        for k, (source, held) in enumerate(
            (
                (matrix_hbm, drift_matrix),
                (offset_hbm, drift_offset),
                (bound_hbm, control_bound),
                (partner_hbm, partner_table),
                (dropped_hbm, dropped_dim),
            )
        )
    ]
    for copy in rim_loads + other_loads:
        copy.start()
    pl.semaphore_wait(barrier, 2 + rank)
    for target in peers:

        @pl.when(rank_of(target) < rank)
        def _():
            pl.semaphore_signal(ready, inc=1, device_id={"sub": target}, device_id_type=pl.DeviceIdType.MESH)


    def rim_copy(step, chunk, way):
        s = chunk // BLOCKS
        cells_sent = pl.ds(PAD + lax.rem(chunk, BLOCKS) * block, block)
        held = first if step == 0 else second
        return pltpu.make_async_remote_copy(
            src_ref=held.at[s, pl.ds(2 + (rows - 2) * (1 - way), 2), :, cells_sent, :],
            dst_ref=held.at[s, pl.ds((rows + 2) * way, 2), :, cells_sent, :],
            send_sem=send_sem.at[step, way, chunk],
            recv_sem=recv_sem.at[step, way, chunk],
            device_id={"gx": lax.rem(at + ring + 1 - 2 * way, ring)},
            device_id_type=pl.DeviceIdType.MESH,
        )

    for copy in rim_loads:
        copy.wait()

    @pl.loop(0, chunks)
    def _(chunk):
        for way in range(2):
            rim_copy(0, chunk, way).start()

    for copy in other_loads:
        copy.wait()

    def repeat_end(held, s, cell, start):
        for r in range(rows):
            for h in range(halves):
                held[s, r + 2, h, pl.ds(start, 2), :] = jnp.broadcast_to(
                    held[s, r + 2, h, pl.ds(cell, 1), :], (2, LANES)
                )

    first_end, last_end = (PAD, PAD - 2), (PAD + cells - 1, PAD + cells)

    @pl.loop(0, subs)
    def _(s):
        repeat_end(first, s, *first_end)
        repeat_end(first, s, *last_end)

    lane = lax.broadcasted_iota(jnp.int32, (TS, LANES), 1)
    at_start = lane == 0
    at_end = lane == LANES - 1
    low_third[...] = jnp.zeros_like(low_third)
    low_second[...] = jnp.full_like(low_second, jnp.inf)

    def coordinate(index, total):
        return -1.0 + (index.astype(jnp.float32) + 0.5) * (2.0 / total)

    def ahead(parts, edge):
        turned = [pltpu.roll(p, LANES - 1, 1) for p in parts]
        return [
            jnp.where(at_end, turned[h + 1] if h + 1 < halves else edge, turned[h])
            for h in range(halves)
        ]

    def behind(parts, edge):
        turned = [pltpu.roll(p, 1, 1) for p in parts]
        return [
            jnp.where(at_start, turned[h - 1] if h > 0 else edge, turned[h]) for h in range(halves)
        ]

    def cells_of(held, step, s, low_row, count, start):
        matrix = [[drift_matrix[d, s, e] * scale[d] for e in range(3)] for d in range(3)]
        offset = [drift_offset[s, d] * scale[d] for d in range(3)]
        bound = [control_bound[s, d] * scale[d] for d in range(3)]
        index = start + lax.broadcasted_iota(jnp.int32, (TS, LANES), 0)
        second_axis = coordinate(index, cells)
        drift_base = []
        for h in range(halves):
            third_axis = coordinate(lane + h * LANES, halves * LANES)
            drift_base.append(
                [matrix[d][1] * second_axis + matrix[d][2] * third_axis for d in range(3)]
            )
        lows = low_third[s, pl.ds(start, TS), :] if step == 1 else None

        def value(r, h, shift=0):
            return held[s, low_row + r + 2, h, pl.ds(PAD + start + shift, TS), :]

        middle = {r: [value(r, h) for h in range(halves)] for r in range(-2, count + 2)}
        along_first = {}
        for h in range(halves):
            slope = {r: middle[r + 1][h] - middle[r][h] for r in range(-2, count + 1)}
            curve = {r: slope[r] - slope[r - 1] for r in range(-1, count + 1)}
            size = {r: jnp.abs(curve[r]) for r in curve}
            for r in range(-1, count):
                face = pick(curve[r], size[r], curve[r + 1], size[r + 1])
                twice = slope[r] + slope[r]
                along_first[r, h, 0] = twice - face
                along_first[r + 1, h, 1] = -(twice + face)
        for r in range(count):
            row = low_row + r
            x0 = -1.0 + ((at * rows + row).astype(jnp.float32) + 0.5) * (2.0 / total_rows)
            center = middle[r]
            up = ahead(center, center[halves - 1])
            down = behind(center, center[0])
            plus = [up[h] - center[h] for h in range(halves)]
            minus = [down[h] - center[h] for h in range(halves)]
            curve = [plus[h] + minus[h] for h in range(halves)]
            curve_up = ahead(curve, 0.0)
            curve_down = behind(curve, 0.0)
            results = []
            for h in range(halves):
                sides = [(along_first[r, h, 0], along_first[r, h, 1])]
                a2, a1, b1, b2 = (value(r, h, k) for k in (-2, -1, 1, 2))
                p = b1 - center[h]
                m = a1 - center[h]
                c = p + m
                c_up = (b2 - b1) - p
                c_down = (a2 - a1) - m
                size, size_up, size_down = jnp.abs(c), jnp.abs(c_up), jnp.abs(c_down)
                sides.append(
                    (
                        (p + p) - pick(c, size, c_up, size_up),
                        (m + m) - pick(c_down, size_down, c, size),
                    )
                )
                c, c_up, c_down = curve[h], curve_up[h], curve_down[h]
                size, size_up, size_down = jnp.abs(c), jnp.abs(c_up), jnp.abs(c_down)
                sides.append(
                    (
                        (plus[h] + plus[h]) - pick(c, size, c_up, size_up),
                        (minus[h] + minus[h]) - pick(c_down, size_down, c, size),
                    )
                )
                drifting = None
                reaching = None
                for d, (x, y) in enumerate(sides):
                    drift = drift_base[h][d] + (offset[d] + matrix[d][0] * x0)
                    term = jnp.abs(drift) * jnp.where(drift >= 0.0, y, x)
                    reach = bound[d] * jnp.maximum(x, y)
                    drifting = term if drifting is None else drifting + term
                    reaching = reach if reaching is None else reaching + reach
                gain = drifting + speed[s, row, h, pl.ds(start, TS), :] * reaching
                result = center[h] + jnp.minimum(gain, 0.0)
                results.append(result)
                if step == 0:
                    second[s, row + 2, h, pl.ds(PAD + start, TS), :] = result
                else:
                    final[s, row, pl.ds(start, TS), pl.ds(h * LANES, LANES)] = result
                    low = result[:8]
                    for k in range(8, TS, 8):
                        low = jnp.minimum(low, result[k : k + 8])
                    low_second[s, row, h] = jnp.minimum(low_second[s, row, h], low)
            if step == 1:
                joint = results[0]
                for part in results[1:]:
                    joint = jnp.minimum(joint, part)
                least = jnp.min(joint, axis=1, keepdims=True)
                lows = jnp.where(lane == row, least, lows)
        if step == 1:
            low_third[s, pl.ds(start, TS), :] = lows

    def run(step, chunk, low_row, count):
        s = chunk // BLOCKS
        j = lax.rem(chunk, BLOCKS) * block

        @pl.loop(0, block // TS)
        def _(t):
            cells_of(
                second if step else first, step, s, low_row, count, pl.multiple_of(j + t * TS, TS)
            )

    def inner(step, chunk):
        run(step, chunk, 2, rows - 4)

    def side(step, chunk, way):
        rim_copy(step, chunk, way).wait_recv()
        run(step, chunk, (rows - 2) * way, 2)
        if step == 0:
            rim_copy(1, chunk, 1 - way).start()

    late = lax.rem(at, LINE) // (LINE // 2)
    early = 1 - late

    @pl.loop(0, LEAD)
    def _(chunk):
        inner(0, chunk)

    @pl.loop(0, chunks + LAG + 1)
    def _(i):
        @pl.when(i + LEAD < chunks)
        def _():
            inner(0, i + LEAD)

        @pl.when(i < chunks)
        def _():
            side(0, i, early)

        @pl.when((i >= LAG) & (i < chunks + LAG))
        def _():
            chunk = i - LAG
            s = chunk // BLOCKS
            side(0, chunk, late)

            @pl.when(lax.rem(chunk, BLOCKS) == 0)
            def _():
                repeat_end(second, s, *first_end)

            @pl.when(lax.rem(chunk, BLOCKS) == BLOCKS - 1)
            def _():
                repeat_end(second, s, *last_end)

        @pl.when(i > LAG)
        def _():
            inner(1, i - LAG - 1)

    def plane_copy(s, k):
        return pltpu.make_async_remote_copy(
            src_ref=own.at[s],
            dst_ref=gathered.at[sub_at * subs + s],
            send_sem=plane_send.at[s, k],
            recv_sem=plane_recv.at[s, k],
            device_id={"sub": peers[k]},
            device_id_type=pl.DeviceIdType.MESH,
        )

    @pl.when(rank < sub_count - 1)
    def _():
        pl.semaphore_wait(ready, sub_count - 1 - rank)

    @pl.loop(0, chunks + LAG)
    def _(i):
        @pl.when(i < chunks)
        def _():
            side(1, i, early)

        @pl.when(i >= LAG)
        def _():
            side(1, i - LAG, late)

        @pl.when((i >= LAG) & (lax.rem(i + BLOCKS - LAG, BLOCKS) == BLOCKS - 1))
        def _():
            s = (i - LAG) // BLOCKS
            over_third = jnp.transpose(low_third[s])[:rows]
            for h in range(halves):
                over_second = jnp.min(low_second[s, :, h], axis=1)
                plane = jnp.where(
                    dropped_dim[s] == 1, over_second, over_third[:, h * LANES : (h + 1) * LANES]
                )
                own[s, :, pl.ds(h * LANES, LANES)] = plane
                gathered[sub_at * subs + s, :, pl.ds(h * LANES, LANES)] = plane
            for k in range(len(peers)):
                plane_copy(s, k).start()

    @pl.loop(0, chunks)
    def _(chunk):
        for step in range(STEPS):
            for way in range(2):
                rim_copy(step, chunk, way).wait_send()

    for s in range(subs):
        for k in range(len(peers)):
            plane_copy(s, k).wait_recv()
    for s in range(subs):
        partner = partner_table[sub_at * subs + s]
        shared_ref[s] = jnp.maximum(own[s], gathered[partner])
    for s in range(subs):
        for k in range(len(peers)):
            plane_copy(s, k).wait_send()


def put_out(final, shared, final_out, shared_out, final_sem, shared_sem):
    subs, rows = final.shape[:2]
    pieces = final_sem.shape[1]
    count = rows // pieces
    copies = [pltpu.make_async_copy(shared, shared_out, shared_sem)]
    for s in range(subs):
        for k in range(pieces):
            at = (s, pl.ds(k * count, count))
            copies.append(pltpu.make_async_copy(final.at[at], final_out.at[at], final_sem.at[s, k]))
    for copy in copies:
        copy.start()
    for copy in copies:
        copy.wait()


def on_device(dims, value_field, speed_field, drift_matrix, *others):
    subs, rows, cells, halves, sub_count, ring, total_rows = dims
    chunks = subs * BLOCKS
    in_vmem = pl.BlockSpec(memory_space=pltpu.VMEM)
    held = pltpu.VMEM((subs, rows + 4, halves, cells + 3 * PAD, LANES), jnp.float32)
    whole = pltpu.VMEM((subs, rows, halves, cells + PAD, LANES), jnp.float32)
    arrays = (value_field, speed_field, jnp.transpose(drift_matrix, (1, 0, 2)), *others)
    results = pl.pallas_call(
        functools.partial(kernel, dims),
        out_shape=(
            jax.ShapeDtypeStruct((subs, rows, cells, halves * LANES), jnp.float32),
            jax.ShapeDtypeStruct((subs, rows, cells), jnp.float32),
        ),
        in_specs=[pl.BlockSpec(memory_space=pltpu.HBM)] * 7,
        out_specs=(in_vmem, in_vmem),
        scratch_shapes=[
            held,
            held,
            whole,
            pltpu.SMEM((3, subs, 3), jnp.float32),
            pltpu.SMEM((subs, 3), jnp.float32),
            pltpu.SMEM((subs, 3), jnp.float32),
            pltpu.SMEM((sub_count * subs,), jnp.int32),
            pltpu.SMEM((subs,), jnp.int32),
            pltpu.VMEM((subs, rows, halves, 8, LANES), jnp.float32),
            pltpu.VMEM((subs, cells, LANES), jnp.float32),
            pltpu.VMEM((subs, rows, cells), jnp.float32),
            pltpu.VMEM((sub_count * subs, rows, cells), jnp.float32),
            pltpu.SemaphoreType.DMA((4, subs, halves)),
            pltpu.SemaphoreType.DMA((5,)),
            pltpu.SemaphoreType.DMA((STEPS, 2, chunks)),
            pltpu.SemaphoreType.DMA((STEPS, 2, chunks)),
            pltpu.SemaphoreType.DMA((subs, sub_count - 1)),
            pltpu.SemaphoreType.DMA((subs, sub_count - 1)),
            pltpu.SemaphoreType.REGULAR,
        ],
        compiler_params=pltpu.CompilerParams(
            collective_id=0, has_side_effects=True, vmem_limit_bytes=40 * 1024 * 1024
        ),
        name="steps_and_planes",
    )(*(pltpu.with_memory_space_constraint(a, pltpu.HBM) for a in arrays))
    return pl.pallas_call(
        put_out,
        out_shape=tuple(jax.ShapeDtypeStruct(r.shape, r.dtype) for r in results),
        in_specs=[pl.BlockSpec(memory_space=pl.ANY)] * 2,
        out_specs=(pl.BlockSpec(memory_space=pl.ANY),) * 2,
        scratch_shapes=[pltpu.SemaphoreType.DMA((subs, 4)), pltpu.SemaphoreType.DMA],
        compiler_params=pltpu.CompilerParams(vmem_limit_bytes=1024 * 1024),
        name="put_out",
    )(*results)


def solution(mesh):
    sub_count, ring = mesh.shape["sub"], mesh.shape["gx"]

    def whole(value_field, *others):
        total_subs, total_rows, cells, third = value_field.shape
        dims = (
            total_subs // sub_count,
            total_rows // ring,
            cells,
            third // LANES,
            sub_count,
            ring,
            total_rows,
        )
        step = jax.shard_map(
            functools.partial(on_device, dims),
            mesh=mesh,
            in_specs=(
                P("sub", "gx", None, None),
                P("sub", "gx", None, None),
                P("sub", None, None),
                P("sub", None),
                P("sub", None),
                P(),
                P("sub"),
            ),
            out_specs=(P("sub", "gx", None, None), P("sub", "gx", None)),
            check_vma=False,
        )
        return step(value_field, *others)

    return whole
```

time: 70.4 us -> 69.4 us (0.986)
  Pallas kernels: 69.7 us -> 68.7 us
    pallas_call x1, Pallas kernels: 67.6 us -> 66.6 us  [on_device(): pl.pallas_call(functools.partial(kernel, dims), out_shape=(jax.ShapeDtype...]
where the time goes in v3:
time: 69.4 us; the launch traced here: 69.3 us
  Pallas kernels  68.7 us (99%)
    pallas_call x1, Pallas kernels, on_device(): pl.pallas_call(functools.partial(kernel, dims), out_shape=(jax.ShapeDtype...  66.6 us
    pallas_call x1, Pallas kernels, on_device(): pl.pallas_call(put_out, out_shape=tuple((jax.ShapeDtypeStruct(r.shape, r....  2.09 us

profile of v3, /device:TPU:1, one launch (start us, length us, event | category | flops | bytes accessed | tf_op | source)
XLA Modules:
  0.0 69.3 jit_solution(521109967100087675)
XLA Ops:
  0.6 66.6 %steps_and_planes.1 = (f32[2,8,256,256]{3,2,1,0:T(8,128)S(1)}, f32[2,8,256]{2,1,0:T(8,128)S(1)}) custom-call(f32[2,8,256,256]{3,2,1,0:T(8,128)} %value_hbm.1, f32[2,8,256,256]{3,2,1,0:T(8,128)} %speed_hbm.1, f32[3,2,3]{2,1,0:T(2,128)} %bitcast.1, f32[2,3]{1,0:T(2,128)} %offset_hbm.1, f32[2,3]{1,0:T(2,128)} %bound_hbm.1, s32[8]{0:T(128)} %partner_hbm.1, ...), custom_call_target="tpu_custom_call" | custom-call | tf_op jit(solution)/shard_map/steps_and_planes/pallas_call | solution.py:401
  67.2 2.1 %put_out.1 = (f32[2,8,256,256]{3,2,1,0:T(8,128)}, f32[2,8,256]{2,1,0:T(8,128)}) custom-call(f32[2,8,256,256]{3,2,1,0:T(8,128)S(1)} %get-tuple-element.4.final, f32[2,8,256]{2,1,0:T(8,128)S(1)} %get-tuple-element.5.shared), custom_call_target="tpu_custom_call" | custom-call | tf_op jit(solution)/shard_map/put_out/pallas_call | solution.py:435

commit v4 on v3

--- a/solution.py
+++ b/solution.py
@@ -82,12 +82,11 @@
     def loads(source, held, spans, first_row, pad, kind):
         return [
             pltpu.make_async_copy(
-                source.at[s, pl.ds(low, count), :, pl.ds(h * LANES, LANES)],
-                held.at[s, pl.ds(first_row + low, count), h, pl.ds(pad, cells), :],
-                load_sem.at[kind + k, s, h],
+                source.at[:, pl.ds(low, count), :, pl.ds(h * LANES, LANES)],
+                held.at[:, pl.ds(first_row + low, count), h, pl.ds(pad, cells), :],
+                load_sem.at[kind + k, h],
             )
             for k, (low, count) in enumerate(spans)
-            for s in range(subs)
             for h in range(halves)
         ]
 
@@ -123,7 +122,7 @@
         return pltpu.make_async_remote_copy(
             src_ref=held.at[s, pl.ds(2 + (rows - 2) * (1 - way), 2), :, cells_sent, :],
             dst_ref=held.at[s, pl.ds((rows + 2) * way, 2), :, cells_sent, :],
-            send_sem=send_sem.at[step, way, chunk],
+            send_sem=send_sem.at[step, way],
             recv_sem=recv_sem.at[step, way, chunk],
             device_id={"gx": lax.rem(at + ring + 1 - 2 * way, ring)},
             device_id_type=pl.DeviceIdType.MESH,
@@ -154,9 +153,6 @@
         repeat_end(first, s, *first_end)
         repeat_end(first, s, *last_end)
 
-    lane = lax.broadcasted_iota(jnp.int32, (TS, LANES), 1)
-    at_start = lane == 0
-    at_end = lane == LANES - 1
     low_third[...] = jnp.zeros_like(low_third)
     low_second[...] = jnp.full_like(low_second, jnp.inf)
 
@@ -164,6 +160,7 @@
         return -1.0 + (index.astype(jnp.float32) + 0.5) * (2.0 / total)
 
     def ahead(parts, edge):
+        at_end = lax.broadcasted_iota(jnp.int32, parts[0].shape, 1) == LANES - 1
         turned = [pltpu.roll(p, LANES - 1, 1) for p in parts]
         return [
             jnp.where(at_end, turned[h + 1] if h + 1 < halves else edge, turned[h])
@@ -171,16 +168,18 @@
         ]
 
     def behind(parts, edge):
+        at_start = lax.broadcasted_iota(jnp.int32, parts[0].shape, 1) == 0
         turned = [pltpu.roll(p, 1, 1) for p in parts]
         return [
             jnp.where(at_start, turned[h - 1] if h > 0 else edge, turned[h]) for h in range(halves)
         ]
 
-    def cells_of(held, step, s, low_row, count, start):
+    def cells_of(held, step, s, low_row, count, start, size_of_block):
         matrix = [[drift_matrix[d, s, e] * scale[d] for e in range(3)] for d in range(3)]
         offset = [drift_offset[s, d] * scale[d] for d in range(3)]
         bound = [control_bound[s, d] * scale[d] for d in range(3)]
-        index = start + lax.broadcasted_iota(jnp.int32, (TS, LANES), 0)
+        lane = lax.broadcasted_iota(jnp.int32, (size_of_block, LANES), 1)
+        index = start + lax.broadcasted_iota(jnp.int32, (size_of_block, LANES), 0)
         second_axis = coordinate(index, cells)
         drift_base = []
         for h in range(halves):
@@ -188,10 +187,10 @@
             drift_base.append(
                 [matrix[d][1] * second_axis + matrix[d][2] * third_axis for d in range(3)]
             )
-        lows = low_third[s, pl.ds(start, TS), :] if step == 1 else None
+        lows = low_third[s, pl.ds(start, size_of_block), :] if step == 1 else None
 
         def value(r, h, shift=0):
-            return held[s, low_row + r + 2, h, pl.ds(PAD + start + shift, TS), :]
+            return held[s, low_row + r + 2, h, pl.ds(PAD + start + shift, size_of_block), :]
 
         middle = {r: [value(r, h) for h in range(halves)] for r in range(-2, count + 2)}
         along_first = {}
@@ -247,15 +246,15 @@
                     reach = bound[d] * jnp.maximum(x, y)
                     drifting = term if drifting is None else drifting + term
                     reaching = reach if reaching is None else reaching + reach
-                gain = drifting + speed[s, row, h, pl.ds(start, TS), :] * reaching
+                gain = drifting + speed[s, row, h, pl.ds(start, size_of_block), :] * reaching
                 result = center[h] + jnp.minimum(gain, 0.0)
                 results.append(result)
                 if step == 0:
-                    second[s, row + 2, h, pl.ds(PAD + start, TS), :] = result
+                    second[s, row + 2, h, pl.ds(PAD + start, size_of_block), :] = result
                 else:
-                    final[s, row, pl.ds(start, TS), pl.ds(h * LANES, LANES)] = result
+                    final[s, row, pl.ds(start, size_of_block), pl.ds(h * LANES, LANES)] = result
                     low = result[:8]
-                    for k in range(8, TS, 8):
+                    for k in range(8, size_of_block, 8):
                         low = jnp.minimum(low, result[k : k + 8])
                     low_second[s, row, h] = jnp.minimum(low_second[s, row, h], low)
             if step == 1:
@@ -265,24 +264,23 @@
                 least = jnp.min(joint, axis=1, keepdims=True)
                 lows = jnp.where(lane == row, least, lows)
         if step == 1:
-            low_third[s, pl.ds(start, TS), :] = lows
-
-    def run(step, chunk, low_row, count):
+            low_third[s, pl.ds(start, size_of_block), :] = lows
+
+    def run(step, chunk, low_row, count, size_of_block):
         s = chunk // BLOCKS
         j = lax.rem(chunk, BLOCKS) * block
 
-        @pl.loop(0, block // TS)
+        @pl.loop(0, block // size_of_block)
         def _(t):
-            cells_of(
-                second if step else first, step, s, low_row, count, pl.multiple_of(j + t * TS, TS)
-            )
+            start = pl.multiple_of(j + t * size_of_block, size_of_block)
+            cells_of(second if step else first, step, s, low_row, count, start, size_of_block)
 
     def inner(step, chunk):
-        run(step, chunk, 2, rows - 4)
+        run(step, chunk, 2, rows - 4, TS)
 
     def side(step, chunk, way):
         rim_copy(step, chunk, way).wait_recv()
-        run(step, chunk, (rows - 2) * way, 2)
+        run(step, chunk, (rows - 2) * way, 2, 2 * TS)
         if step == 0:
             rim_copy(1, chunk, 1 - way).start()
 
@@ -359,11 +357,17 @@
             for k in range(len(peers)):
                 plane_copy(s, k).start()
 
-    @pl.loop(0, chunks)
-    def _(chunk):
-        for step in range(STEPS):
-            for way in range(2):
-                rim_copy(step, chunk, way).wait_send()
+    for step in range(STEPS):
+        for way in range(2):
+            every = (first if step == 0 else second).at[:, pl.ds(2, 2), :, pl.ds(PAD, cells), :]
+            pltpu.make_async_remote_copy(
+                src_ref=every,
+                dst_ref=every,
+                send_sem=send_sem.at[step, way],
+                recv_sem=recv_sem.at[step, way, 0],
+                device_id={"gx": right},
+                device_id_type=pl.DeviceIdType.MESH,
+            ).wait_send()
 
     for s in range(subs):
         for k in range(len(peers)):
@@ -419,9 +423,9 @@
             pltpu.VMEM((subs, cells, LANES), jnp.float32),
             pltpu.VMEM((subs, rows, cells), jnp.float32),
             pltpu.VMEM((sub_count * subs, rows, cells), jnp.float32),
-            pltpu.SemaphoreType.DMA((4, subs, halves)),
+            pltpu.SemaphoreType.DMA((4, halves)),
             pltpu.SemaphoreType.DMA((5,)),
-            pltpu.SemaphoreType.DMA((STEPS, 2, chunks)),
+            pltpu.SemaphoreType.DMA((STEPS, 2)),
             pltpu.SemaphoreType.DMA((STEPS, 2, chunks)),
             pltpu.SemaphoreType.DMA((subs, sub_count - 1)),
             pltpu.SemaphoreType.DMA((subs, sub_count - 1)),

time: 69.4 us -> 68.5 us (0.987)
  Pallas kernels: 68.7 us -> 67.8 us
    pallas_call x1, Pallas kernels: 66.6 us -> 65.7 us  [on_device(): pl.pallas_call(functools.partial(kernel, dims), out_shape=(jax.ShapeDtype...]
where the time goes in v4:
time: 68.5 us; the launch traced here: 68.4 us
  Pallas kernels  67.8 us (99%)
    pallas_call x1, Pallas kernels, on_device(): pl.pallas_call(functools.partial(kernel, dims), out_shape=(jax.ShapeDtype...  65.7 us
    pallas_call x1, Pallas kernels, on_device(): pl.pallas_call(put_out, out_shape=tuple((jax.ShapeDtypeStruct(r.shape, r....  2.09 us

profile of v4, /device:TPU:1, one launch (start us, length us, event | category | flops | bytes accessed | tf_op | source)
XLA Modules:
  0.0 68.4 jit_solution(4104432018010455956)
XLA Ops:
  0.6 65.7 %steps_and_planes.1 = (f32[2,8,256,256]{3,2,1,0:T(8,128)S(1)}, f32[2,8,256]{2,1,0:T(8,128)S(1)}) custom-call(f32[2,8,256,256]{3,2,1,0:T(8,128)} %value_hbm.1, f32[2,8,256,256]{3,2,1,0:T(8,128)} %speed_hbm.1, f32[3,2,3]{2,1,0:T(2,128)} %bitcast.1, f32[2,3]{1,0:T(2,128)} %offset_hbm.1, f32[2,3]{1,0:T(2,128)} %bound_hbm.1, s32[8]{0:T(128)} %partner_hbm.1, ...), custom_call_target="tpu_custom_call" | custom-call | tf_op jit(solution)/shard_map/steps_and_planes/pallas_call | solution.py:405
  66.3 2.1 %put_out.1 = (f32[2,8,256,256]{3,2,1,0:T(8,128)}, f32[2,8,256]{2,1,0:T(8,128)}) custom-call(f32[2,8,256,256]{3,2,1,0:T(8,128)S(1)} %get-tuple-element.4.final, f32[2,8,256]{2,1,0:T(8,128)S(1)} %get-tuple-element.5.shared), custom_call_target="tpu_custom_call" | custom-call | tf_op jit(solution)/shard_map/put_out/pallas_call | solution.py:439

commit v5 on v4

--- a/solution.py
+++ b/solution.py
@@ -12,7 +12,7 @@
 PAD = 8
 TS = 16
 LINE = 4
-LAG = 2
+LAG = 1
 LEAD = 6
 BLOCKS = 8
 

time: 68.5 us -> 68.5 us (level)
  no operation moved by 1% of the time
where the time goes in v5:
time: 68.5 us; the launch traced here: 68.4 us
  Pallas kernels  67.8 us (99%)
    pallas_call x1, Pallas kernels, on_device(): pl.pallas_call(functools.partial(kernel, dims), out_shape=(jax.ShapeDtype...  65.7 us
    pallas_call x1, Pallas kernels, on_device(): pl.pallas_call(put_out, out_shape=tuple((jax.ShapeDtypeStruct(r.shape, r....  2.09 us

profile of v5, /device:TPU:1, one launch (start us, length us, event | category | flops | bytes accessed | tf_op | source)
XLA Modules:
  0.0 68.4 jit_solution(16169246915099269198)
XLA Ops:
  0.6 65.7 %steps_and_planes.1 = (f32[2,8,256,256]{3,2,1,0:T(8,128)S(1)}, f32[2,8,256]{2,1,0:T(8,128)S(1)}) custom-call(f32[2,8,256,256]{3,2,1,0:T(8,128)} %value_hbm.1, f32[2,8,256,256]{3,2,1,0:T(8,128)} %speed_hbm.1, f32[3,2,3]{2,1,0:T(2,128)} %bitcast.1, f32[2,3]{1,0:T(2,128)} %offset_hbm.1, f32[2,3]{1,0:T(2,128)} %bound_hbm.1, s32[8]{0:T(128)} %partner_hbm.1, ...), custom_call_target="tpu_custom_call" | custom-call | tf_op jit(solution)/shard_map/steps_and_planes/pallas_call | solution.py:405
  66.3 2.1 %put_out.1 = (f32[2,8,256,256]{3,2,1,0:T(8,128)}, f32[2,8,256]{2,1,0:T(8,128)}) custom-call(f32[2,8,256,256]{3,2,1,0:T(8,128)S(1)} %get-tuple-element.4.final, f32[2,8,256]{2,1,0:T(8,128)S(1)} %get-tuple-element.5.shared), custom_call_target="tpu_custom_call" | custom-call | tf_op jit(solution)/shard_map/put_out/pallas_call | solution.py:439
